TPU v7x, 32 devices: a whole 2x2x4 slice. The times are simulated.
32 devices in a mesh: batch: 16 (over z, y, x), cols: 2 (over core).
Axes of the slice: x: 2, y: 2, z: 4, core: 2. Of those that a mesh axis runs over, the one named last changes fastest.
Arguments:
- grad_up: float32 [16, 1024, 4096], P('batch', None, 'cols'), may hold values from -0.875 to 0.875
- grad_down: float32 [16, 4096, 1024], P('batch', 'cols'), may hold values from -0.875 to 0.875
- grad_query: float32 [16, 1024, 1024], P('batch', None, 'cols'), may hold values from -0.875 to 0.875
- grad_key: float32 [16, 1024, 1024], P('batch', None, 'cols'), may hold values from -0.875 to 0.875
- grad_value: float32 [16, 1024, 1024], P('batch', None, 'cols'), may hold values from -0.875 to 0.875
- grad_mixed: float32 [16, 1024, 1024], P('batch', 'cols'), may hold values from -0.875 to 0.875
- grad_norm: float32 [16, 1024], P('batch'), may hold values from -8 to 8
- weight_up: float32 [1024, 4096], P('batch', 'cols'), may hold values from -0.1875 to 0.1875
- weight_down: float32 [4096, 1024], P('cols', 'batch'), may hold values from -0.09375 to 0.09375
- weight_query: float32 [1024, 1024], P('batch', 'cols'), may hold values from -0.1875 to 0.1875
- weight_key: float32 [1024, 1024], P('batch', 'cols'), may hold values from -0.1875 to 0.1875
- weight_value: float32 [1024, 1024], P('batch', 'cols'), may hold values from -0.1875 to 0.1875
- weight_mixed: float32 [1024, 1024], P('cols', 'batch'), may hold values from -0.1875 to 0.1875
- weight_norm: float32 [1024], P('batch'), may hold values from 0.25 to 1.75
Outputs:
- copy_up: bfloat16 [1024, 4096], P(None, 'cols')
- copy_down: bfloat16 [4096, 1024], P('cols')
- copy_query: bfloat16 [1024, 1024], P(None, 'cols')
- copy_key: bfloat16 [1024, 1024], P(None, 'cols')
- copy_value: bfloat16 [1024, 1024], P(None, 'cols')
- copy_mixed: bfloat16 [1024, 1024], P('cols')
- copy_norm: bfloat16 [1024], replicated
- new_up: float32 [1024, 4096], P('batch', 'cols')
- new_down: float32 [4096, 1024], P('cols', 'batch')
- new_query: float32 [1024, 1024], P('batch', 'cols')
- new_key: float32 [1024, 1024], P('batch', 'cols')
- new_value: float32 [1024, 1024], P('batch', 'cols')
- new_mixed: float32 [1024, 1024], P('cols', 'batch')
- new_norm: float32 [1024], P('batch')
All inputs are finite; a program needn't handle non-finite values.
Results may differ from a plain program's by a relative error of at most 0.0004.
Values may be sent and summed in bfloat16 or wider, within the bound.
A program may use at most 128 MiB of HBM per device.

v0:
```python
import jax
import jax.numpy as jnp
from jax import lax
from jax.sharding import PartitionSpec as P

learn_rate = 0.3


def shards(
    grad_up,
    grad_down,
    grad_query,
    grad_key,
    grad_value,
    grad_mixed,
    grad_norm,
    weight_up,
    weight_down,
    weight_query,
    weight_key,
    weight_value,
    weight_mixed,
    weight_norm,
):
    mean_up, mean_down, mean_query, mean_key, mean_value, mean_mixed, mean_norm = (
        lax.psum_scatter(grad_up[0], "batch", scatter_dimension=0, tiled=True),
        lax.psum_scatter(grad_down[0], "batch", scatter_dimension=1, tiled=True),
        lax.psum_scatter(grad_query[0], "batch", scatter_dimension=0, tiled=True),
        lax.psum_scatter(grad_key[0], "batch", scatter_dimension=0, tiled=True),
        lax.psum_scatter(grad_value[0], "batch", scatter_dimension=0, tiled=True),
        lax.psum_scatter(grad_mixed[0], "batch", scatter_dimension=1, tiled=True),
        lax.psum_scatter(grad_norm[0], "batch", scatter_dimension=0, tiled=True),
    )
    mean_rate = lax.axis_size("batch") ** (-0.5)
    mean_up = mean_up * mean_rate
    mean_down = mean_down * mean_rate
    mean_query = mean_query * mean_rate
    mean_key = mean_key * mean_rate
    mean_value = mean_value * mean_rate
    mean_mixed = mean_mixed * mean_rate
    mean_norm = mean_norm * mean_rate
    new_up = weight_up - learn_rate * mean_up
    new_down = weight_down - learn_rate * mean_down
    new_query = weight_query - learn_rate * mean_query
    new_key = weight_key - learn_rate * mean_key
    new_value = weight_value - learn_rate * mean_value
    new_mixed = weight_mixed - learn_rate * mean_mixed
    new_norm = weight_norm - learn_rate * mean_norm
    copy_up, copy_down, copy_query, copy_key, copy_value, copy_mixed, copy_norm = (
        lax.all_gather(new_up.astype(jnp.bfloat16), "batch", axis=0, tiled=True),
        lax.all_gather(new_down.astype(jnp.bfloat16), "batch", axis=1, tiled=True),
        lax.all_gather(new_query.astype(jnp.bfloat16), "batch", axis=0, tiled=True),
        lax.all_gather(new_key.astype(jnp.bfloat16), "batch", axis=0, tiled=True),
        lax.all_gather(new_value.astype(jnp.bfloat16), "batch", axis=0, tiled=True),
        lax.all_gather(new_mixed.astype(jnp.bfloat16), "batch", axis=1, tiled=True),
        lax.all_gather(new_norm.astype(jnp.bfloat16), "batch", axis=0, tiled=True),
    )
    return (
        copy_up,
        copy_down,
        copy_query,
        copy_key,
        copy_value,
        copy_mixed,
        copy_norm,
        new_up,
        new_down,
        new_query,
        new_key,
        new_value,
        new_mixed,
        new_norm,
    )


def solution(mesh):
    placed = (
        P("batch", None, "cols"),
        P("batch", "cols", None),
        P("batch", None, "cols"),
        P("batch", None, "cols"),
        P("batch", None, "cols"),
        P("batch", "cols", None),
        P("batch", None),
        P("batch", "cols"),
        P("cols", "batch"),
        P("batch", "cols"),
        P("batch", "cols"),
        P("batch", "cols"),
        P("cols", "batch"),
        P("batch"),
    )
    return jax.shard_map(
        shards,
        mesh=mesh,
        in_specs=placed,
        out_specs=(
            P(None, "cols"),
            P("cols", None),
            P(None, "cols"),
            P(None, "cols"),
            P(None, "cols"),
            P("cols", None),
            P(),
            P("batch", "cols"),
            P("cols", "batch"),
            P("batch", "cols"),
            P("batch", "cols"),
            P("batch", "cols"),
            P("cols", "batch"),
            P("batch"),
        ),
        check_vma=False,
    )
```

profile of v0, /device:TPU:0, one launch (start us, length us, event | category | flops | bytes accessed | tf_op | source)
XLA Modules:
  0.0 1104.0 jit_solution(16749740426630674211)
XLA Ops:
  7.2 0.0 reduce-scatter.11.cloned.1.call-start
  7.2 0.7 reduce-scatter.11.cloned.1.call-update
  7.9 0.0 reduce-scatter.13.cloned.1.call-start
  8.0 0.7 reduce-scatter.13.cloned.1.call-update
  8.7 0.0 reduce-scatter.15.cloned.1.call-start
  8.7 0.7 reduce-scatter.15.cloned.1.call-update
  9.4 0.0 reduce-scatter.17.cloned.1.call-start
  9.5 1.8 copy.33
  11.3 0.0 reduce-scatter.17.cloned.1.call-update
  11.3 0.0 reduce-scatter.7.cloned.1.call-start
  11.4 0.5 reduce-scatter.7.cloned.1.call-update
  11.9 0.0 reduce-scatter.9.cloned.1.call-start
  11.9 9.2 copy.32
  21.2 0.0 reduce-scatter.9.cloned.1.call-update
  21.3 0.0 all-gather.11.cloned.1.call-start
  21.3 73.1 %reduce-scatter.11.cloned.1.call-done = f32[64,512]{1,0:T(8,128)} async-done(((f32[1024,512]{1,0:T(8,128)}), f32[64,512]{1,0:T(8,128)}) %reduce-scatter.11.cloned.1.call-update) | async-done | bytes 131088 | tf_op jit(solution)/shard_map/reduce_scatter | solution.py:28
  94.5 1.6 fusion.6
  96.1 0.0 all-gather.13.cloned.1.call-start
  96.1 78.7 %reduce-scatter.13.cloned.1.call-done = f32[64,512]{1,0:T(8,128)} async-done(((f32[1024,512]{1,0:T(8,128)}), f32[64,512]{1,0:T(8,128)}) %reduce-scatter.13.cloned.1.call-update) | async-done | bytes 131088 | tf_op jit(solution)/shard_map/reduce_scatter | solution.py:29
  174.8 1.6 fusion.5
  176.4 0.0 all-gather.15.cloned.1.call-start
  176.5 78.7 %reduce-scatter.15.cloned.1.call-done = f32[64,512]{1,0:T(8,128)} async-done(((f32[1024,512]{1,0:T(8,128)}), f32[64,512]{1,0:T(8,128)}) %reduce-scatter.15.cloned.1.call-update) | async-done | bytes 131088 | tf_op jit(solution)/shard_map/reduce_scatter | solution.py:30
  255.2 1.6 fusion.4
  256.8 0.0 all-gather.17.cloned.1.call-start
  256.8 79.2 %reduce-scatter.17.cloned.1.call-done = f32[512,64]{0,1:T(8,128)} async-done(((f32[512,1024]{0,1:T(8,128)}), f32[512,64]{0,1:T(8,128)}) %reduce-scatter.17.cloned.1.call-update) | async-done | bytes 131088 | tf_op jit(solution)/shard_map/reduce_scatter | solution.py:31
  336.0 1.6 fusion.3
  337.6 0.0 all-gather.7.cloned.1.call-start
  337.7 174.8 %reduce-scatter.7.cloned.1.call-done = f32[64,2048]{1,0:T(8,128)} async-done(((f32[1024,2048]{1,0:T(8,128)}), f32[64,2048]{1,0:T(8,128)}) %reduce-scatter.7.cloned.1.call-update) | async-done | bytes 524304 | tf_op jit(solution)/shard_map/reduce_scatter | solution.py:26
  512.5 2.0 fusion.8
  514.5 0.0 all-gather.9.cloned.1.call-start
  514.5 180.4 %reduce-scatter.9.cloned.1.call-done = f32[2048,64]{0,1:T(8,128)} async-done(((f32[2048,1024]{0,1:T(8,128)}), f32[2048,64]{0,1:T(8,128)}) %reduce-scatter.9.cloned.1.call-update) | async-done | bytes 524304 | tf_op jit(solution)/shard_map/reduce_scatter | solution.py:27
  695.0 2.0 fusion.7
  697.0 0.6 fusion.9
  698.9 42.5 %all-reduce.1 = f32[1024]{0:T(1024)S(1)} all-reduce(f32[1024]{0:T(1024)S(1)} %bitcast.15), channel_id=8, replica_groups=mesh['batch'=16,'cols'=2] {'batch'}, use_global_device_ids=true, to_apply=%region_6.0.clone | all-reduce | flops 1024 | bytes 8192
  741.4 0.6 fusion.1
  742.0 0.2 dynamic-update-slice
  742.2 37.3 %all-reduce = bf16[1024]{0:T(1024)(128)(2,1)} all-reduce(bf16[1024]{0:T(1024)(128)(2,1)S(1)} %dynamic-update-slice), channel_id=1, replica_groups=mesh['batch'=16,'cols'=2] {'batch'}, use_global_device_ids=true, to_apply=%add | all-reduce | flops 1024 | bytes 4096
  779.5 33.8 %all-gather.13.cloned.1.call-done = bf16[1024,512]{1,0:T(8,128)(2,1)} async-done(((bf16[64,512]{1,0:T(8,128)(2,1)}), bf16[1024,512]{1,0:T(8,128)(2,1)}) %all-gather.13.cloned.1.call-update) | async-done | bytes 1048592 | tf_op jit(solution)/shard_map/all_gather | solution.py:53
  813.3 57.3 %all-gather.15.cloned.1.call-done = bf16[1024,512]{1,0:T(8,128)(2,1)} async-done(((bf16[64,512]{1,0:T(8,128)(2,1)}), bf16[1024,512]{1,0:T(8,128)(2,1)}) %all-gather.15.cloned.1.call-update) | async-done | bytes 1048592 | tf_op jit(solution)/shard_map/all_gather | solution.py:54
  870.6 57.1 %all-gather.17.cloned.1.call-done = bf16[512,1024]{0,1:T(8,128)(2,1)} async-done(((bf16[512,64]{0,1:T(8,128)(2,1)}), bf16[512,1024]{0,1:T(8,128)(2,1)}) %all-gather.17.cloned.1.call-update) | async-done | bytes 1048592 | tf_op jit(solution)/shard_map/all_gather | solution.py:55
  927.7 2.3 copy.35
  930.0 75.5 %all-gather.7.cloned.1.call-done = bf16[1024,2048]{1,0:T(8,128)(2,1)} async-done(((bf16[64,2048]{1,0:T(8,128)(2,1)}), bf16[1024,2048]{1,0:T(8,128)(2,1)}) %all-gather.7.cloned.1.call-update) | async-done | bytes 4194320 | tf_op jit(solution)/shard_map/all_gather | solution.py:50
  1005.5 77.4 %all-gather.9.cloned.1.call-done = bf16[2048,1024]{0,1:T(8,128)(2,1)} async-done(((bf16[2048,64]{0,1:T(8,128)(2,1)}), bf16[2048,1024]{0,1:T(8,128)(2,1)}) %all-gather.9.cloned.1.call-update) | async-done | bytes 4194320 | tf_op jit(solution)/shard_map/all_gather | solution.py:51
  1082.9 6.4 copy.34
  1089.3 4.9 copy.41
  1094.3 1.0 copy.42
  1095.3 1.0 copy.43
  1096.2 1.0 copy.44
  (34 shorter events, 0.2 us)
Async XLA Ops:
  7.2 2.3 copy-start
  7.2 87.3 %reduce-scatter.11.cloned.1.call-start = ((), (), s32[]{:S(2)}) async-start(), calls=%async_computation.10 | async-start | bytes 2228224 | tf_op jit(solution)/shard_map/reduce_scatter | solution.py:28
  7.9 166.9 %reduce-scatter.13.cloned.1.call-start = ((), (), s32[]{:S(2)}) async-start(), calls=%async_computation.12 | async-start | bytes 2228224 | tf_op jit(solution)/shard_map/reduce_scatter | solution.py:29
  8.7 246.5 %reduce-scatter.15.cloned.1.call-start = ((), (), s32[]{:S(2)}) async-start(), calls=%async_computation.14 | async-start | bytes 2228224 | tf_op jit(solution)/shard_map/reduce_scatter | solution.py:30
  9.4 326.6 %reduce-scatter.17.cloned.1.call-start = ((), (), s32[]{:S(2)}) async-start(), calls=%async_computation.16 | async-start | bytes 2228224 | tf_op jit(solution)/shard_map/reduce_scatter | solution.py:31
  11.3 501.2 %reduce-scatter.7.cloned.1.call-start = ((), (), s32[]{:S(2)}) async-start(), calls=%async_computation.6 | async-start | bytes 8912896 | tf_op jit(solution)/shard_map/reduce_scatter | solution.py:26
  11.9 683.1 %reduce-scatter.9.cloned.1.call-start = ((), (), s32[]{:S(2)}) async-start(), calls=%async_computation.8 | async-start | bytes 8912896 | tf_op jit(solution)/shard_map/reduce_scatter | solution.py:27
  21.2 73.3 %copy-start.6 = (f32[64,512]{1,0:T(8,128)S(1)}, f32[64,512]{1,0:T(8,128)}, u32[]{:S(2)}) copy-start(f32[64,512]{1,0:T(8,128)} %param.23) | copy-start | bytes 393220
  21.2 153.6 %copy-start.7 = (f32[64,512]{1,0:T(8,128)S(1)}, f32[64,512]{1,0:T(8,128)}, u32[]{:S(2)}) copy-start(f32[64,512]{1,0:T(8,128)} %param.24) | copy-start | bytes 393220
  21.2 234.0 %copy-start.8 = (f32[64,512]{1,0:T(8,128)S(1)}, f32[64,512]{1,0:T(8,128)}, u32[]{:S(2)}) copy-start(f32[64,512]{1,0:T(8,128)} %param.25) | copy-start | bytes 393220
  21.2 314.8 %copy-start.9 = (f32[512,64]{0,1:T(8,128)S(1)}, f32[512,64]{0,1:T(8,128)}, u32[]{:S(2)}) copy-start(f32[512,64]{0,1:T(8,128)} %param.26) | copy-start | bytes 393220
  21.2 491.3 %copy-start.4 = (f32[64,2048]{1,0:T(8,128)S(1)}, f32[64,2048]{1,0:T(8,128)}, u32[]{:S(2)}) copy-start(f32[64,2048]{1,0:T(8,128)} %param.21) | copy-start | bytes 1572868
  21.2 673.8 %copy-start.5 = (f32[2048,64]{0,1:T(8,128)S(1)}, f32[2048,64]{0,1:T(8,128)}, u32[]{:S(2)}) copy-start(f32[2048,64]{0,1:T(8,128)} %param.22) | copy-start | bytes 1572868
  21.2 675.8 %copy-start.11 = (u32[32]{0:T(128)S(1)}, u32[32]{0:T(128)}, u32[]{:S(2)}) copy-start(u32[32]{0:T(128)} %constant.27) | copy-start | bytes 388
  21.2 677.7 %copy-start.10 = (f32[1,1024]{1,0:T(1,128)S(1)}, f32[1,1024]{1,0:T(1,128)}, u32[]{:S(2)}) copy-start(f32[1,1024]{1,0:T(1,128)} %param.20) | copy-start | bytes 12292
  21.3 720.1 %copy-start.12 = (f32[64]{0:T(128)S(1)}, f32[64]{0:T(128)}, u32[]{:S(2)}) copy-start(f32[64]{0:T(128)} %param.27) | copy-start | bytes 772
  21.3 758.2 %all-gather.11.cloned.1.call-start = ((), (), s32[]{:S(2)}) async-start(), calls=%async_computation.11 | async-start | bytes 1114112 | tf_op jit(solution)/shard_map/all_gather | solution.py:52
  96.1 717.2 %all-gather.13.cloned.1.call-start = ((), (), s32[]{:S(2)}) async-start(), calls=%async_computation.13 | async-start | bytes 1114112 | tf_op jit(solution)/shard_map/all_gather | solution.py:53
  176.4 694.2 %all-gather.15.cloned.1.call-start = ((), (), s32[]{:S(2)}) async-start(), calls=%async_computation.15 | async-start | bytes 1114112 | tf_op jit(solution)/shard_map/all_gather | solution.py:54
  256.8 670.9 %all-gather.17.cloned.1.call-start = ((), (), s32[]{:S(2)}) async-start(), calls=%async_computation.17 | async-start | bytes 1114112 | tf_op jit(solution)/shard_map/all_gather | solution.py:55
  337.6 667.9 %all-gather.7.cloned.1.call-start = ((), (), s32[]{:S(2)}) async-start(), calls=%async_computation.7 | async-start | bytes 4456448 | tf_op jit(solution)/shard_map/all_gather | solution.py:50
  514.5 568.5 %all-gather.9.cloned.1.call-start = ((), (), s32[]{:S(2)}) async-start(), calls=%async_computation.9 | async-start | bytes 4456448 | tf_op jit(solution)/shard_map/all_gather | solution.py:51
  1089.3 4.9 copy-start.1
  1089.3 5.9 copy-start.2
  1094.3 1.9 copy-start.3
Sparse Core Ops, SparseCore 0:
  10.3 84.1 reduce-scatter.10
  96.7 78.0 reduce-scatter.12
  177.1 78.0 reduce-scatter.14
  257.9 78.0 reduce-scatter.16
  338.2 174.2 reduce-scatter.6
  514.6 180.3 reduce-scatter.8
  698.3 57.5 all-gather.10
  759.3 53.9 all-gather.12
  816.6 53.9 all-gather.14
  873.8 53.9 all-gather.16
  931.1 74.4 all-gather.6
  1008.7 74.1 all-gather.8
where the time goes:
time: 1100 us
  waiting for transfers between devices  969 us (88%)
  blocking collectives  79.8 us (7%)
  local copies, waits for them, and re-layouts  28.4 us (3%)
  between operations  15.6 us (1%)
    reduce_scatter x1, waiting for transfers between devices, shards(): lax.psum_scatter(grad_down[0], 'batch', scatter_dimension=1, tiled=True)  180 us
    reduce_scatter x1, waiting for transfers between devices, shards(): lax.psum_scatter(grad_up[0], 'batch', scatter_dimension=0, tiled=True)  175 us
    unnamed x2, blocking collectives  79.8 us
    reduce_scatter x1, waiting for transfers between devices, shards(): lax.psum_scatter(grad_mixed[0], 'batch', scatter_dimension=1, tiled=True)  79.2 us
    reduce_scatter x1, waiting for transfers between devices, shards(): lax.psum_scatter(grad_value[0], 'batch', scatter_dimension=0, tiled=True)  78.7 us
    reduce_scatter x1, waiting for transfers between devices, shards(): lax.psum_scatter(grad_key[0], 'batch', scatter_dimension=0, tiled=True)  78.7 us
    all_gather x1, waiting for transfers between devices, shards(): lax.all_gather(new_down.astype(jnp.bfloat16), 'batch', axis=1, tiled=True)  77.4 us
    all_gather x1, waiting for transfers between devices, shards(): lax.all_gather(new_up.astype(jnp.bfloat16), 'batch', axis=0, tiled=True)  75.5 us
  transfers between devices with their start and end apart: 12, of which 11 were waited for; matrix products, arithmetic and copies ran while one was open for 2% of the time, Pallas kernels for 0%

commit v1 on v0

--- a/solution.py
+++ b/solution.py
@@ -48,7 +48,7 @@
     new_norm = weight_norm - learn_rate * mean_norm
     copy_up, copy_down, copy_query, copy_key, copy_value, copy_mixed, copy_norm = (
         lax.all_gather(new_up.astype(jnp.bfloat16), "batch", axis=0, tiled=True),
-        lax.all_gather(new_down.astype(jnp.bfloat16), "batch", axis=1, tiled=True),
+        jnp.concatenate(lax.all_gather(new_down.astype(jnp.bfloat16), "batch"), axis=1),
         lax.all_gather(new_query.astype(jnp.bfloat16), "batch", axis=0, tiled=True),
         lax.all_gather(new_key.astype(jnp.bfloat16), "batch", axis=0, tiled=True),
         lax.all_gather(new_value.astype(jnp.bfloat16), "batch", axis=0, tiled=True),

time: 1100 us -> 1100 us (level)
  waiting for transfers between devices: 969 us -> 954 us
    all_gather x1, waiting for transfers between devices: 75.5 us -> 62 us  [shards(): lax.all_gather(new_up.astype(jnp.bfloat16), 'batch', axis=0, tiled=True)]
    unnamed x37 -> x38, local copies, waits for them, and re-layouts: 28.4 us -> 33 us
  transfers between devices with their start and end apart: 12 -> 12, of which waited for: 11 -> 11; matrix products, arithmetic and copies ran while one was open for 2% -> 4% of each run, Pallas kernels for 0% -> 0%
where the time goes in v1:
time: 1100 us
  waiting for transfers between devices  954 us (87%)
  blocking collectives  79.8 us (7%)
  local copies, waits for them, and re-layouts  37.3 us (3%)
  between operations  15.6 us (1%)
    reduce_scatter x1, waiting for transfers between devices, shards(): lax.psum_scatter(grad_up[0], 'batch', scatter_dimension=0, tiled=True)  180 us
    reduce_scatter x1, waiting for transfers between devices, shards(): lax.psum_scatter(grad_down[0], 'batch', scatter_dimension=1, tiled=True)  175 us
    unnamed x2, blocking collectives  79.8 us
    reduce_scatter x1, waiting for transfers between devices, shards(): lax.psum_scatter(grad_mixed[0], 'batch', scatter_dimension=1, tiled=True)  79.3 us
    reduce_scatter x1, waiting for transfers between devices, shards(): lax.psum_scatter(grad_key[0], 'batch', scatter_dimension=0, tiled=True)  78.7 us
    reduce_scatter x1, waiting for transfers between devices, shards(): lax.psum_scatter(grad_value[0], 'batch', scatter_dimension=0, tiled=True)  78.4 us
    all_gather x1, waiting for transfers between devices, shards(): lax.all_gather(new_down.astype(jnp.bfloat16), 'batch')  76.2 us
    reduce_scatter x1, waiting for transfers between devices, shards(): lax.psum_scatter(grad_query[0], 'batch', scatter_dimension=0, tiled=True)  73.3 us
  transfers between devices with their start and end apart: 12, of which 11 were waited for; matrix products, arithmetic and copies ran while one was open for 4% of the time, Pallas kernels for 0%

profile of v1, /device:TPU:0, one launch (start us, length us, event | category | flops | bytes accessed | tf_op | source)
XLA Modules:
  0.0 1098.1 jit_solution(13457386707055419796)
XLA Ops:
  7.2 0.0 reduce-scatter.11.cloned.1.call-start
  7.2 0.7 reduce-scatter.11.cloned.1.call-update
  7.9 0.0 reduce-scatter.13.cloned.1.call-start
  8.0 0.7 reduce-scatter.13.cloned.1.call-update
  8.7 0.0 reduce-scatter.15.cloned.1.call-start
  8.7 0.7 reduce-scatter.15.cloned.1.call-update
  9.4 0.0 reduce-scatter.17.cloned.1.call-start
  9.5 1.8 copy.43
  11.3 0.0 reduce-scatter.9.cloned.1.call-start
  11.4 9.2 copy.41
  20.6 0.0 reduce-scatter.7.cloned.1.call-start
  20.7 0.5 reduce-scatter.7.cloned.1.call-update
  21.2 0.0 all-gather.10.cloned.1.call-start
  21.3 73.3 %reduce-scatter.11.cloned.1.call-done = f32[64,512]{1,0:T(8,128)} async-done(((f32[1024,512]{1,0:T(8,128)}), f32[64,512]{1,0:T(8,128)}) %reduce-scatter.11.cloned.1.call-update) | async-done | bytes 131088 | tf_op jit(solution)/shard_map/reduce_scatter | solution.py:28
  94.5 1.6 fusion.6
  96.2 0.0 all-gather.12.cloned.1.call-start
  96.2 78.7 %reduce-scatter.13.cloned.1.call-done = f32[64,512]{1,0:T(8,128)} async-done(((f32[1024,512]{1,0:T(8,128)}), f32[64,512]{1,0:T(8,128)}) %reduce-scatter.13.cloned.1.call-update) | async-done | bytes 131088 | tf_op jit(solution)/shard_map/reduce_scatter | solution.py:29
  174.9 1.6 fusion.5
  176.6 0.0 all-gather.14.cloned.1.call-start
  176.6 78.4 %reduce-scatter.15.cloned.1.call-done = f32[64,512]{1,0:T(8,128)} async-done(((f32[1024,512]{1,0:T(8,128)}), f32[64,512]{1,0:T(8,128)}) %reduce-scatter.15.cloned.1.call-update) | async-done | bytes 131088 | tf_op jit(solution)/shard_map/reduce_scatter | solution.py:30
  255.0 1.6 fusion.4
  256.7 0.0 all-gather.16.cloned.1.call-start
  256.7 79.3 %reduce-scatter.17.cloned.1.call-done = f32[512,64]{0,1:T(8,128)} async-done(((f32[512,1024]{0,1:T(8,128)}), f32[512,64]{0,1:T(8,128)}) %reduce-scatter.17.cloned.1.call-update) | async-done | bytes 131088 | tf_op jit(solution)/shard_map/reduce_scatter | solution.py:31
  336.0 1.6 fusion.3
  337.7 0.0 all-gather.18.cloned.1.call-start
  337.7 174.8 %reduce-scatter.9.cloned.1.call-done = f32[2048,64]{0,1:T(8,128)} async-done(((f32[2048,1024]{0,1:T(8,128)}), f32[2048,64]{0,1:T(8,128)}) %reduce-scatter.9.cloned.1.call-update) | async-done | bytes 524304 | tf_op jit(solution)/shard_map/reduce_scatter | solution.py:27
  512.5 2.0 fusion.7
  514.5 0.0 all-gather.8.cloned.1.call-start
  514.5 180.4 %reduce-scatter.7.cloned.1.call-done = f32[64,2048]{1,0:T(8,128)} async-done(((f32[1024,2048]{1,0:T(8,128)}), f32[64,2048]{1,0:T(8,128)}) %reduce-scatter.7.cloned.1.call-update) | async-done | bytes 524304 | tf_op jit(solution)/shard_map/reduce_scatter | solution.py:26
  694.9 2.0 fusion.8
  697.0 0.6 fusion.9
  698.9 42.5 %all-reduce.1 = f32[1024]{0:T(1024)S(1)} all-reduce(f32[1024]{0:T(1024)S(1)} %bitcast.25), channel_id=9, replica_groups=mesh['batch'=16,'cols'=2] {'batch'}, use_global_device_ids=true, to_apply=%region_6.0.clone | all-reduce | flops 1024 | bytes 8192
  741.4 0.6 fusion.1
  742.0 0.2 dynamic-update-slice
  742.1 37.3 %all-reduce = bf16[1024]{0:T(1024)(128)(2,1)} all-reduce(bf16[1024]{0:T(1024)(128)(2,1)S(1)} %dynamic-update-slice), channel_id=1, replica_groups=mesh['batch'=16,'cols'=2] {'batch'}, use_global_device_ids=true, to_apply=%add | all-reduce | flops 1024 | bytes 4096
  779.5 33.8 %all-gather.12.cloned.1.call-done = bf16[1024,512]{1,0:T(8,128)(2,1)} async-done(((bf16[64,512]{1,0:T(8,128)(2,1)}), bf16[1024,512]{1,0:T(8,128)(2,1)}) %all-gather.12.cloned.1.call-update) | async-done | bytes 1048592 | tf_op jit(solution)/shard_map/all_gather | solution.py:53
  813.3 57.3 %all-gather.14.cloned.1.call-done = bf16[1024,512]{1,0:T(8,128)(2,1)} async-done(((bf16[64,512]{1,0:T(8,128)(2,1)}), bf16[1024,512]{1,0:T(8,128)(2,1)}) %all-gather.14.cloned.1.call-update) | async-done | bytes 1048592 | tf_op jit(solution)/shard_map/all_gather | solution.py:54
  870.5 57.1 %all-gather.16.cloned.1.call-done = bf16[512,1024]{0,1:T(8,128)(2,1)} async-done(((bf16[512,64]{0,1:T(8,128)(2,1)}), bf16[512,1024]{0,1:T(8,128)(2,1)}) %all-gather.16.cloned.1.call-update) | async-done | bytes 1048592 | tf_op jit(solution)/shard_map/all_gather | solution.py:55
  927.7 2.3 copy.45
  929.9 76.2 %all-gather.18.cloned.1.call-done = bf16[32768,64]{0,1:T(8,128)(2,1)} async-done(((bf16[2048,64]{0,1:T(8,128)(2,1)}), bf16[32768,64]{0,1:T(8,128)(2,1)}) %all-gather.18.cloned.1.call-update) | async-done | bytes 4194320 | tf_op jit(solution)/shard_map/all_gather | solution.py:51
  1006.1 4.6 copy.46
  1010.7 4.3 copy.42
  1015.0 6.4 copy.44
  1021.4 62.0 %all-gather.8.cloned.1.call-done = bf16[1024,2048]{1,0:T(8,128)(2,1)} async-done(((bf16[64,2048]{1,0:T(8,128)(2,1)}), bf16[1024,2048]{1,0:T(8,128)(2,1)}) %all-gather.8.cloned.1.call-update) | async-done | bytes 4194320 | tf_op jit(solution)/shard_map/all_gather | solution.py:50
  1083.4 4.9 copy.52
  1088.4 1.0 copy.53
  1089.3 1.0 copy.54
  1090.3 1.0 copy.55
  (36 shorter events, 0.2 us)
Async XLA Ops:
  7.2 2.3 copy-start
  7.2 87.4 %reduce-scatter.11.cloned.1.call-start = ((), (), s32[]{:S(2)}) async-start(), calls=%async_computation.9 | async-start | bytes 2228224 | tf_op jit(solution)/shard_map/reduce_scatter | solution.py:28
  7.9 167.0 %reduce-scatter.13.cloned.1.call-start = ((), (), s32[]{:S(2)}) async-start(), calls=%async_computation.11 | async-start | bytes 2228224 | tf_op jit(solution)/shard_map/reduce_scatter | solution.py:29
  8.7 246.4 %reduce-scatter.15.cloned.1.call-start = ((), (), s32[]{:S(2)}) async-start(), calls=%async_computation.13 | async-start | bytes 2228224 | tf_op jit(solution)/shard_map/reduce_scatter | solution.py:30
  9.4 326.6 %reduce-scatter.17.cloned.1.call-start = ((), (), s32[]{:S(2)}) async-start(), calls=%async_computation.15 | async-start | bytes 2228224 | tf_op jit(solution)/shard_map/reduce_scatter | solution.py:31
  11.3 501.2 %reduce-scatter.9.cloned.1.call-start = ((), (), s32[]{:S(2)}) async-start(), calls=%async_computation.8 | async-start | bytes 8912896 | tf_op jit(solution)/shard_map/reduce_scatter | solution.py:27
  20.6 674.3 %reduce-scatter.7.cloned.1.call-start = ((), (), s32[]{:S(2)}) async-start(), calls=%async_computation.6 | async-start | bytes 8912896 | tf_op jit(solution)/shard_map/reduce_scatter | solution.py:26
  20.6 73.9 %copy-start.6 = (f32[64,512]{1,0:T(8,128)S(1)}, f32[64,512]{1,0:T(8,128)}, u32[]{:S(2)}) copy-start(f32[64,512]{1,0:T(8,128)} %param.23) | copy-start | bytes 393220
  20.7 154.3 %copy-start.7 = (f32[64,512]{1,0:T(8,128)S(1)}, f32[64,512]{1,0:T(8,128)}, u32[]{:S(2)}) copy-start(f32[64,512]{1,0:T(8,128)} %param.24) | copy-start | bytes 393220
  20.7 234.4 %copy-start.8 = (f32[64,512]{1,0:T(8,128)S(1)}, f32[64,512]{1,0:T(8,128)}, u32[]{:S(2)}) copy-start(f32[64,512]{1,0:T(8,128)} %param.25) | copy-start | bytes 393220
  20.7 315.4 %copy-start.9 = (f32[512,64]{0,1:T(8,128)S(1)}, f32[512,64]{0,1:T(8,128)}, u32[]{:S(2)}) copy-start(f32[512,64]{0,1:T(8,128)} %param.26) | copy-start | bytes 393220
  20.7 491.8 %copy-start.4 = (f32[2048,64]{0,1:T(8,128)S(1)}, f32[2048,64]{0,1:T(8,128)}, u32[]{:S(2)}) copy-start(f32[2048,64]{0,1:T(8,128)} %param.22) | copy-start | bytes 1572868
  21.2 673.8 %copy-start.5 = (f32[64,2048]{1,0:T(8,128)S(1)}, f32[64,2048]{1,0:T(8,128)}, u32[]{:S(2)}) copy-start(f32[64,2048]{1,0:T(8,128)} %param.21) | copy-start | bytes 1572868
  21.2 675.8 %copy-start.11 = (u32[32]{0:T(128)S(1)}, u32[32]{0:T(128)}, u32[]{:S(2)}) copy-start(u32[32]{0:T(128)} %constant.27) | copy-start | bytes 388
  21.2 677.6 %copy-start.10 = (f32[1,1024]{1,0:T(1,128)S(1)}, f32[1,1024]{1,0:T(1,128)}, u32[]{:S(2)}) copy-start(f32[1,1024]{1,0:T(1,128)} %param.20) | copy-start | bytes 12292
  21.2 720.2 %copy-start.12 = (f32[64]{0:T(128)S(1)}, f32[64]{0:T(128)}, u32[]{:S(2)}) copy-start(f32[64]{0:T(128)} %param.27) | copy-start | bytes 772
  21.2 758.2 %all-gather.10.cloned.1.call-start = ((), (), s32[]{:S(2)}) async-start(), calls=%async_computation.10 | async-start | bytes 1114112 | tf_op jit(solution)/shard_map/all_gather | solution.py:52
  96.2 717.1 %all-gather.12.cloned.1.call-start = ((), (), s32[]{:S(2)}) async-start(), calls=%async_computation.12 | async-start | bytes 1114112 | tf_op jit(solution)/shard_map/all_gather | solution.py:53
  176.6 694.0 %all-gather.14.cloned.1.call-start = ((), (), s32[]{:S(2)}) async-start(), calls=%async_computation.14 | async-start | bytes 1114112 | tf_op jit(solution)/shard_map/all_gather | solution.py:54
  256.7 671.0 %all-gather.16.cloned.1.call-start = ((), (), s32[]{:S(2)}) async-start(), calls=%async_computation.16 | async-start | bytes 1114112 | tf_op jit(solution)/shard_map/all_gather | solution.py:55
  337.7 668.4 %all-gather.18.cloned.1.call-start = ((), (), s32[]{:S(2)}) async-start(), calls=%async_computation.17 | async-start | bytes 4456448 | tf_op jit(solution)/shard_map/all_gather | solution.py:51
  514.5 568.9 %all-gather.8.cloned.1.call-start = ((), (), s32[]{:S(2)}) async-start(), calls=%async_computation.7 | async-start | bytes 4456448 | tf_op jit(solution)/shard_map/all_gather | solution.py:50
  1083.4 4.9 copy-start.1
  1083.4 5.9 copy-start.2
  1088.4 1.9 copy-start.3
Sparse Core Ops, SparseCore 0:
  10.3 84.2 reduce-scatter.10
  96.8 78.0 reduce-scatter.12
  177.2 77.7 reduce-scatter.14
  257.7 78.2 reduce-scatter.16
  338.2 174.2 reduce-scatter.8
  514.6 180.2 reduce-scatter.6
  698.3 57.6 all-gather.9
  759.2 53.9 all-gather.11
  816.6 53.9 all-gather.13
  873.7 53.9 all-gather.15
  931.0 75.0 all-gather.17
  1009.3 74.0 all-gather.7
